TPU v7x, 32 devices: a whole 2x2x4 slice. The times are simulated.
32 devices in a mesh: owner: 4 (over x, core), rows: 8 (over z, y).
Axes of the slice: x: 2, y: 2, z: 4, core: 2. Of those that a mesh axis runs over, the one named last changes fastest.
Arguments:
- master_down: float32 [8, 14336, 4096], P('owner', None, 'rows'), may hold values from -0.046875 to 0.046875
- router_weight: float32 [4096, 8], P('rows', 'owner'), may hold values from -0.09375 to 0.09375
- router_gain: float32 [4096], P('rows'), may hold values from 0.25 to 1.75
Outputs:
- final_down: bfloat16 [8, 4096, 14336], P('owner', None, 'rows')
- serve_router: bfloat16 [4096, 8], replicated
All inputs are finite; a program needn't handle non-finite values.
Results may differ from a plain program's by a relative error of at most 0.001.
Values may be sent and summed in bfloat16 or wider, within the bound.
No kernel may reach another device: no remote copies, remote signals or barrier semaphores. Data moves between devices by JAX's collectives and lax.ppermute only.
A program may use at most 192 MiB of HBM per device.

v0:
```python
import jax
import jax.numpy as jnp
from jax import lax
from jax.sharding import PartitionSpec as P


def shards(master_down, router_weight, router_gain):
    turned_down = jnp.transpose(master_down, (0, 2, 1))
    narrow_down = turned_down.astype(jnp.bfloat16)
    final_down = lax.all_to_all(narrow_down, "rows", split_axis=2, concat_axis=1, tiled=True)
    part_router = (router_weight * router_gain[:, None]).astype(jnp.bfloat16)
    row_router = lax.all_gather(part_router, "rows", axis=0, tiled=True)
    serve_router = lax.all_gather(row_router, "owner", axis=1, tiled=True)
    return (final_down, serve_router)


def solution(mesh):
    return jax.shard_map(
        shards,
        mesh=mesh,
        in_specs=(P("owner", None, "rows"), P("rows", "owner"), P("rows")),
        out_specs=(P("owner", None, "rows"), P()),
        check_vma=False,
    )
```

profile of v0, /device:TPU:0, one launch (start us, length us, event | category | flops | bytes accessed | tf_op | source)
XLA Modules:
  0.0 817.2 jit_solution(17658122797674117112)
XLA Ops:
  0.6 28.5 %convert_element_type.12 = bf16[2,14336,512]{2,1,0:T(8,128)(2,1)} convert(f32[2,14336,512]{2,1,0:T(8,128)} %param.3) | non-fusion elementwise | flops 14680064 | bytes 88080384 | tf_op jit(solution)/shard_map/convert_element_type | solution.py:9
  29.1 52.8 %copy.10 = bf16[2,14336,512]{2,0,1:T(2,128)(2,1)} copy(bf16[2,14336,512]{2,1,0:T(8,128)(2,1)} %convert_element_type.12) | data formatting | bytes 58720256
  81.9 0.0 copy-start
  81.9 0.0 copy-start.1
  81.9 7.5 all-to-all-start
  89.4 0.0 copy-done
  89.4 0.0 copy-done.1
  89.4 652.0 %all_gather.6 = bf16[4096,2]{0,1:T(2,128)(2,1)S(1)} all-gather(bf16[512,2]{0,1:T(2,128)(2,1)S(1)} %multiply_convert_fusion), channel_id=1, replica_groups=mesh['owner'=4,'rows'=8] {'rows'}, dimensions={0}, use_global_device_ids=true | all-gather | bytes 18432 | tf_op jit(solution)/shard_map/all_gather | solution.py:12
  741.4 5.2 all-gather
  746.6 0.7 reshape.6
  747.2 0.0 all-to-all-done
  747.3 70.0 %copy.7 = bf16[2,8,512,1792]{3,2,1,0:T(8,128)(2,1)} copy(bf16[2,8,512,1792]{2,0,3,1:T(2,128)(2,1)} %bitcast.2) | data formatting | bytes 58720256 | tf_op jit(solution)/shard_map/all_to_all | solution.py:10
  (1 shorter events, 0.0 us)
Async XLA Ops:
  81.9 7.5 copy-start
  81.9 7.5 copy-start.1
  81.9 665.3 %all-to-all-start = ((bf16[2,512,14336]{1,0,2:T(2,128)(2,1)}), bf16[2,512,14336]{1,0,2:T(2,128)(2,1)}, u32[]{:S(2)}, u32[]{:S(2)}) async-start(bf16[2,512,14336]{1,0,2:T(2,128)(2,1)} %bitcast.11), calls=%async_computation | async-start | bytes 58720256 | tf_op jit(solution)/shard_map/all_to_all | solution.py:10
where the time goes:
time: 819 us; the launch traced here: 817 us
  blocking collectives  657 us (80%)
  local copies, waits for them, and re-layouts  123 us (15%)
  other arithmetic  28.5 us (3%)
    all_gather x1, blocking collectives, shards(): row_router = lax.all_gather(part_router, 'rows', axis=0, tiled=True)  652 us
    all_to_all x1, local copies, waits for them, and re-layouts, shards(): lax.all_to_all(narrow_down, 'rows', split_axis=2, concat_axis=1, tiled=True)  70 us
    unnamed x6, local copies, waits for them, and re-layouts  53.5 us
    convert_element_type x1, other arithmetic, shards(): narrow_down = turned_down.astype(jnp.bfloat16)  28.5 us
  transfers between devices with their start and end apart: 1, of which 0 were waited for; matrix products, arithmetic and copies ran while one was open for 0% of the time, Pallas kernels for 0%

commit v1 on v0

--- a/solution.py
+++ b/solution.py
@@ -7,7 +7,11 @@
 def shards(master_down, router_weight, router_gain):
     turned_down = jnp.transpose(master_down, (0, 2, 1))
     narrow_down = turned_down.astype(jnp.bfloat16)
-    final_down = lax.all_to_all(narrow_down, "rows", split_axis=2, concat_axis=1, tiled=True)
+    placed = lax.axis_size("rows")
+    z1 = jnp.split(narrow_down, placed, 2)
+    response = jnp.stack(z1, 0)
+    arr_out = lax.all_to_all(response, "rows", 0, 0)
+    final_down = jnp.concatenate(arr_out, 1)
     part_router = (router_weight * router_gain[:, None]).astype(jnp.bfloat16)
     row_router = lax.all_gather(part_router, "rows", axis=0, tiled=True)
     serve_router = lax.all_gather(row_router, "owner", axis=1, tiled=True)

time: 819 us -> 765 us (0.934)
  local copies, waits for them, and re-layouts: 123 us -> 69.4 us
    all_to_all x1 -> x0, local copies, waits for them, and re-layouts: 70 us -> none  [shards(): lax.all_to_all(narrow_down, 'rows', split_axis=2, concat_axis=1, tiled=True)]
    reshape x0 -> x1, local copies, waits for them, and re-layouts: none -> 36 us  [shards(): final_down = jnp.concatenate(arr_out, 1)]
    unnamed x6 -> x12, local copies, waits for them, and re-layouts: 53.5 us -> 29.4 us
where the time goes in v1:
time: 765 us; the launch traced here: 763 us
  blocking collectives  657 us (86%)
  local copies, waits for them, and re-layouts  69.4 us (9%)
  other arithmetic  28.5 us (4%)
    all_gather x1, blocking collectives, shards(): row_router = lax.all_gather(part_router, 'rows', axis=0, tiled=True)  652 us
    reshape x1, local copies, waits for them, and re-layouts, shards(): final_down = jnp.concatenate(arr_out, 1)  36 us
    unnamed x12, local copies, waits for them, and re-layouts  29.4 us
    convert_element_type x1, other arithmetic, shards(): narrow_down = turned_down.astype(jnp.bfloat16)  28.5 us
  transfers between devices with their start and end apart: 1, of which 0 were waited for; matrix products, arithmetic and copies ran while one was open for 0% of the time, Pallas kernels for 0%

profile of v1, /device:TPU:0, one launch (start us, length us, event | category | flops | bytes accessed | tf_op | source)
XLA Modules:
  0.0 763.2 jit_solution(5256674096772135787)
XLA Ops:
  0.6 28.5 %convert_bitcast_fusion = bf16[2,512,14336]{1,2,0:T(8,128)(2,1)} fusion(f32[2,14336,512]{2,1,0:T(8,128)} %param.3), kind=kLoop, calls=%fused_computation | loop fusion | flops 14680064 | bytes 88080384 | tf_op jit(solution)/shard_map/convert_element_type | solution.py:9
  29.1 4.1 fusion.7
  33.1 4.1 fusion.6
  37.2 4.1 fusion.5
  41.3 4.1 fusion.4
  45.4 4.2 fusion.3
  49.6 4.1 fusion.2
  53.6 4.2 fusion.1
  57.8 4.1 fusion
  61.9 0.0 copy-start
  61.9 0.0 copy-start.1
  61.9 7.4 all-to-all-start
  69.3 0.0 copy-done
  69.3 0.0 copy-done.1
  69.4 652.0 %all_gather.6 = bf16[4096,2]{0,1:T(2,128)(2,1)S(1)} all-gather(bf16[512,2]{0,1:T(2,128)(2,1)S(1)} %multiply_convert_fusion), channel_id=1, replica_groups=mesh['owner'=4,'rows'=8] {'rows'}, dimensions={0}, use_global_device_ids=true | all-gather | bytes 18432 | tf_op jit(solution)/shard_map/all_gather | solution.py:16
  721.3 5.2 all-gather
  726.6 0.7 reshape.14
  727.2 0.0 all-to-all-done
  727.2 36.0 %copy.6 = bf16[2,8,512,1792]{3,2,1,0:T(8,128)(2,1)} copy(bf16[2,8,512,1792]{2,3,0,1:T(8,128)(2,1)} %bitcast.9) | data formatting | bytes 58720256 | tf_op jit(solution)/shard_map/reshape | solution.py:14
  (1 shorter events, 0.0 us)
Async XLA Ops:
  61.9 7.4 copy-start
  61.9 7.5 copy-start.1
  61.9 665.3 %all-to-all-start = ((bf16[8,2,512,1792]{2,3,1,0:T(8,128)(2,1)}), bf16[8,2,512,1792]{2,3,1,0:T(8,128)(2,1)}, u32[]{:S(2)}, u32[]{:S(2)}) async-start(bf16[8,2,512,1792]{2,3,1,0:T(8,128)(2,1)} %fusion), calls=%async_computation | async-start | bytes 58720256 | tf_op jit(solution)/shard_map/all_to_all | solution.py:13
